TPU v7x, 32 devices: a whole 2x2x4 slice. The times are simulated.
32 devices in a mesh: dp: 4 (over y, x), samp: 4 (over z), col: 2 (over core).
Axes of the slice: x: 2, y: 2, z: 4, core: 2. Of those that a mesh axis runs over, the one named last changes fastest.
Arguments:
- looked_rows: bfloat16 [16, 1920, 128], P(('dp', 'samp'), None, 'col'), may hold values from -6 to 6
- bag_ids: int32 [16, 1920], P(('dp', 'samp')), may hold values from 0 to 959, never falling along the last dimension, each value on 1 to 4 neighbouring positions
- slot_of: int32 [40], replicated, may hold values from 0 to 39, each once
- labels: int32 [384], P(('dp', 'samp')), may hold values 0 or 1
- out_weight: bfloat16 [3, 128], replicated, may hold values from -0.02734375 to 0.02734375
- filter_first: bfloat16 [128, 1521], replicated, may hold values from -0.15625 to 0.15625
- filter_second: bfloat16 [128, 4992], replicated, may hold values from -0.078125 to 0.078125
- filter_third: bfloat16 [128, 4992], replicated, may hold values from -0.078125 to 0.078125
Outputs:
- row_grads: bfloat16 [16, 1920, 128], P(('dp', 'samp'), None, 'col')
- grad_first: float32 [128, 1521], P('dp')
- grad_second: float32 [128, 4992], P('dp')
- grad_third: float32 [128, 4992], P('dp')
Inputs may be any that keep to these rules, and one draw needn't show every extreme that they name: `bag_ids`: within each owner's row, bag numbers never fall; each of the 960 bags has 1 to 4 entries and some bag exactly 4. `slot_of`: each slot number once.
All inputs are finite; a program needn't handle non-finite values. No bound on the sum of `labels` on one device may be relied on, other than what follows from the above.
Results may differ from a plain program's by a relative error of at most 0.014.
Values may be sent and summed in bfloat16 or wider, within the bound.
No kernel may reach another device: no remote copies, remote signals or barrier semaphores. Data moves between devices by JAX's collectives and lax.ppermute only.
A program may use at most 64 MiB of HBM per device.

v0:
```python
import jax
import jax.numpy as jnp
from jax import lax
from jax.sharding import PartitionSpec as P

FIELDS = 39
loss_scale = 16.0
block_rows = 4


def outer_block(previous, anchor):
    spread_rows = previous.astype(jnp.float32)[:, None, :] * anchor.astype(jnp.float32)[None, :, :]
    return spread_rows.astype(jnp.bfloat16)


def forward_layer(filter_cube, previous, anchor):

    def one_block(operands):
        outer_products = outer_block(operands[0], operands[1])
        projected_maps = jnp.einsum(
            "ocf,cfl->ol", filter_cube, outer_products, preferred_element_type=jnp.float32
        )
        return projected_maps.astype(jnp.bfloat16)

    return lax.map(one_block, (previous, anchor))


def backward_layer(filter_cube, cotangent, previous, anchor):

    def accumulate(running, operands):
        cotangent_part, previous_block, anchor_block = operands
        outer_products = outer_block(previous_block, anchor_block)
        running = running + jnp.einsum(
            "ol,cfl->ocf", cotangent_part, outer_products, preferred_element_type=jnp.float32
        )
        spread_rows = jnp.einsum(
            "ocf,ol->cfl", filter_cube, cotangent_part, preferred_element_type=jnp.float32
        )
        grad_previous = jnp.sum(spread_rows * anchor_block.astype(jnp.float32)[None, :, :], axis=1)
        grad_anchor = jnp.sum(spread_rows * previous_block.astype(jnp.float32)[:, None, :], axis=0)
        return (running, (grad_previous, grad_anchor))

    starting = jnp.zeros(filter_cube.shape, jnp.float32)
    running, (grad_previous, grad_anchor) = lax.scan(
        accumulate, starting, (cotangent, previous, anchor)
    )
    return (
        running.reshape(filter_cube.shape[0], filter_cube.shape[1] * filter_cube.shape[2]),
        grad_previous,
        grad_anchor,
    )


def local(
    looked_rows, bag_ids, slot_of, labels, out_weight, filter_first, filter_second, filter_third
):
    samples = labels.shape[0]
    slots = slot_of.shape[0]
    bag_count = samples * slots
    owners = lax.axis_size("samp")
    group_size = samples * owners
    slot_span = slots // owners
    blocks = samples // block_rows
    entries = bag_ids[0]
    member = (entries[None, :] == jnp.arange(bag_count, dtype=jnp.int32)[:, None]).astype(
        jnp.bfloat16
    )
    pooled = jnp.dot(member, looked_rows[0], preferred_element_type=jnp.float32).astype(
        jnp.bfloat16
    )
    width = pooled.shape[1]
    lanes = block_rows * width
    pooled = pooled.reshape(group_size, slot_span, width)
    arrived = lax.all_to_all(pooled, "samp", split_axis=0, concat_axis=1, tiled=True)
    chooser = (slot_of[:FIELDS][:, None] == jnp.arange(slots, dtype=jnp.int32)[None, :]).astype(
        jnp.bfloat16
    )
    arrived_blocks = arrived.reshape(blocks, block_rows, slots, width)
    anchor = jnp.einsum(
        "fk,nbkd->nfbd", chooser, arrived_blocks, preferred_element_type=jnp.float32
    ).astype(jnp.bfloat16)
    anchor = anchor.reshape(blocks, FIELDS, lanes)
    cube_first = filter_first.reshape(filter_first.shape[0], FIELDS, FIELDS)
    cube_second = filter_second.reshape(
        filter_second.shape[0], filter_second.shape[1] // FIELDS, FIELDS
    )
    cube_third = filter_third.reshape(
        filter_third.shape[0], filter_third.shape[1] // FIELDS, FIELDS
    )
    maps_count = filter_first.shape[0]
    layer_one = forward_layer(cube_first, anchor, anchor)
    layer_two = forward_layer(cube_second, layer_one, anchor)
    layer_three = forward_layer(cube_third, layer_two, anchor)

    def column_sums(layer):
        summed = jnp.sum(
            layer.astype(jnp.float32).reshape(blocks, maps_count, block_rows, width), axis=3
        )
        return summed.transpose(0, 2, 1).reshape(samples, maps_count)

    maps_one, maps_two, maps_three = lax.psum(
        (column_sums(layer_one), column_sums(layer_two), column_sums(layer_three)), "col"
    )
    weights_out = out_weight.astype(jnp.float32)
    logits = jnp.dot(maps_one, weights_out[0], precision=lax.Precision.HIGHEST)
    logits = logits + jnp.dot(maps_two, weights_out[1], precision=lax.Precision.HIGHEST)
    logits = logits + jnp.dot(maps_three, weights_out[2], precision=lax.Precision.HIGHEST)
    residual_slope = loss_scale * (jax.nn.sigmoid(logits) - labels.astype(jnp.float32))

    def direct_term(weight_row):
        scaled = (residual_slope[:, None] * weight_row[None, :]).reshape(
            blocks, block_rows, maps_count
        )
        scaled = scaled.transpose(0, 2, 1)[:, :, :, None]
        return jnp.broadcast_to(scaled, (blocks, maps_count, block_rows, width)).reshape(
            blocks, maps_count, lanes
        )

    cotan_three = direct_term(weights_out[2]).astype(jnp.bfloat16)
    grad_three, back_two, base_three = backward_layer(cube_third, cotan_three, layer_two, anchor)
    cotan_two = (direct_term(weights_out[1]) + back_two).astype(jnp.bfloat16)
    grad_two, back_one, base_two = backward_layer(cube_second, cotan_two, layer_one, anchor)
    cotan_one = (direct_term(weights_out[0]) + back_one).astype(jnp.bfloat16)
    grad_one, back_zero, base_one = backward_layer(cube_first, cotan_one, anchor, anchor)
    grad_fields = (back_zero + base_one + base_two + base_three).astype(jnp.bfloat16)
    grad_fields = grad_fields.reshape(blocks, FIELDS, block_rows, width)
    slot_grads = jnp.einsum(
        "fk,nfbd->nbkd", chooser, grad_fields, preferred_element_type=jnp.float32
    ).astype(jnp.bfloat16)
    slot_grads = slot_grads.reshape(samples, slots, width)
    returned = lax.all_to_all(slot_grads, "samp", split_axis=1, concat_axis=0, tiled=True)
    bag_grads = returned.reshape(bag_count, width)
    row_grads = jnp.einsum(
        "be,bd->ed", member, bag_grads, preferred_element_type=jnp.float32
    ).astype(jnp.bfloat16)
    shares = (
        lax.psum_scatter(
            grad_one.astype(jnp.bfloat16), "dp", scatter_dimension=0, tiled=True
        ).astype(jnp.float32),
        lax.psum_scatter(
            grad_two.astype(jnp.bfloat16), "dp", scatter_dimension=0, tiled=True
        ).astype(jnp.float32),
        lax.psum_scatter(
            grad_three.astype(jnp.bfloat16), "dp", scatter_dimension=0, tiled=True
        ).astype(jnp.float32),
    )
    summed = (
        lax.psum(shares[0].astype(jnp.bfloat16), ("samp", "col")).astype(jnp.float32),
        lax.psum(shares[1].astype(jnp.bfloat16), ("samp", "col")).astype(jnp.float32),
        lax.psum(shares[2].astype(jnp.bfloat16), ("samp", "col")).astype(jnp.float32),
    )
    return (row_grads[None], summed[0], summed[1], summed[2])


def solution(mesh):
    in_specs = (
        P(("dp", "samp"), None, "col"),
        P(("dp", "samp"), None),
        P(),
        P(("dp", "samp")),
        P(),
        P(),
        P(),
        P(),
    )
    out_specs = (P(("dp", "samp"), None, "col"), P("dp", None), P("dp", None), P("dp", None))
    return jax.shard_map(local, mesh=mesh, in_specs=in_specs, out_specs=out_specs, check_vma=False)
```

profile of v0, /device:TPU:0, one launch (start us, length us, event | category | flops | bytes accessed | tf_op | source)
XLA Modules:
  0.0 423.8 jit_solution(5831816907563971014)
XLA Ops:
  10.8 6.3 %all-to-all-start = ((bf16[4,2,7680]{2,1,0:T(2,128)(2,1)}), bf16[4,2,7680]{2,1,0:T(2,128)(2,1)S(1)}, u32[]{:S(2)}, u32[]{:S(2)}) async-start(bf16[4,2,7680]{2,1,0:T(2,128)(2,1)} %reshape.218), calls=%async_computation | async-start | bytes 245760 | tf_op jit(solution)/shard_map/all_to_all | solution.py:74
  32.3 9.0 %while.75 = (s32[]{:T(128)}, bf16[6,128,256]{1,2,0:T(8,128)(2,1)S(1)}, bf16[6,39,256]{2,1,0:T(8,128)(2,1)S(1)}, bf16[128,39,39]{0,2,1:T(8,128)(2,1)}, s32[]{:T(128)}) while((s32[]{:T(128)}, bf16[6,128,256]{1,2,0:T(8,128)(2,1)S(1)}, bf16[6,39,256]{2,1,0:T(8,128)(2,1)S(1)}, bf16[128,39,39]{0,2,1:T(8,128)(2,1)}, s32[]{:T(128)}) %tuple.131), condition=%wide.region_1.2_spmd, body=%wide.region_0.1_spmd.sunk | while | flops 100501760 | bytes 596805 | solution.py:25
  42.2 20.9 %while.76 = (s32[]{:T(128)}, bf16[6,128,256]{1,2,0:T(8,128)(2,1)}, bf16[6,128,256]{1,2,0:T(8,128)(2,1)S(1)}, bf16[6,39,256]{2,1,0:T(8,128)(2,1)S(1)}, bf16[128,128,39]{1,0,2:T(8,128)(2,1)}, /*index=5*/s32[]{:T(128)}) while((s32[]{:T(128)}, bf16[6,128,256]{1,2,0:T(8,128)(2,1)}, bf16[6,128,256]{1,2,0:T(8,128)(2,1)S(1)}, ...), condition=%wide.region_5.6_spmd, body=%wide.region_4.5_spmd.sunk | while | flops 329787136 | bytes 1771597 | solution.py:25
  42.2 3.5 fusion.114
  45.7 3.5 fusion.114
  49.2 3.5 fusion.114
  52.7 3.5 fusion.114
  56.2 3.5 fusion.114
  59.6 3.5 fusion.114
  65.0 25.9 %while.77 = (s32[]{:T(128)}, bf16[6,128,256]{1,2,0:T(8,128)(2,1)}, bf16[6,128,256]{1,2,0:T(8,128)(2,1)}, bf16[6,39,256]{2,1,0:T(8,128)(2,1)S(1)}, bf16[128,128,39]{1,0,2:T(8,128)(2,1)}, /*index=5*/s32[]{:T(128)}) while((s32[]{:T(128)}, bf16[6,128,256]{1,2,0:T(8,128)(2,1)}, bf16[6,128,256]{1,2,0:T(8,128)(2,1)}, ...), condition=%wide.region_9.10_spmd, body=%wide.region_8.9_spmd.sunk | while | flops 329787136 | bytes 1771597 | solution.py:25
  65.9 3.5 fusion.116
  70.2 3.4 fusion.116
  74.5 3.4 fusion.116
  78.8 3.4 fusion.116
  83.2 3.5 fusion.116
  87.5 3.4 fusion.116
  92.0 3.7 all-reduce
  99.4 60.1 %while.78 = (s32[]{:T(128)}, f32[128,128,39]{1,0,2:T(8,128)}, f32[6,128,256]{1,2,0:T(8,128)}, f32[6,39,256]{2,1,0:T(8,128)}, bf16[6,128,256]{1,2,0:T(8,128)(2,1)...) while((s32[]{:T(128)}, f32[128,128,39]{1,0,2:T(8,128)}, ...), condition=%wide.region_15.16_spmd.clone, body=%wide.region_12.15_spmd.clone.sunk | while | flops 663257088 | bytes 13271699 | solution.py:44
  100.4 3.4 select_add_fusion.4
  103.8 2.5 fusion.119
  109.7 4.3 %select_add_fusion.4 = f32[128,128,39]{1,0,2:T(8,128)} fusion(f32[128,128,39]{1,0,2:T(8,128)} %get-tuple-element.797, f32[39,256]{1,0:T(8,128)S(1)} %bitcast_convert_fusion.25, f32[128,256]{1,0:T(8,128)S(1)} %bitcast_convert_fusion.26, pred[]{:T(512)S(6)} %compare.9, bf16[6,128,256]{1,2,0:T(8,128)(2,1)} %get-tuple-element.810, s32[]{:T(128)} %get-tuple-element.796), kind=kOutput, calls=%fused_computation.34.clone.1 | convolution fusion | flops 330989568 | bytes 5348865 | tf_op jit(solution)/shard_map/while/body/eval_jaxpr/ol,cfl->ocf/dot_general | solution.py:33
  114.0 2.5 fusion.119
  119.8 4.3 %select_add_fusion.4 = f32[128,128,39]{1,0,2:T(8,128)} fusion(f32[128,128,39]{1,0,2:T(8,128)} %get-tuple-element.797, f32[39,256]{1,0:T(8,128)S(1)} %bitcast_convert_fusion.25, f32[128,256]{1,0:T(8,128)S(1)} %bitcast_convert_fusion.26, pred[]{:T(512)S(6)} %compare.9, bf16[6,128,256]{1,2,0:T(8,128)(2,1)} %get-tuple-element.810, s32[]{:T(128)} %get-tuple-element.796), kind=kOutput, calls=%fused_computation.34.clone.1 | convolution fusion | flops 330989568 | bytes 5348865 | tf_op jit(solution)/shard_map/while/body/eval_jaxpr/ol,cfl->ocf/dot_general | solution.py:33
  124.2 2.5 fusion.119
  130.0 4.3 %select_add_fusion.4 = f32[128,128,39]{1,0,2:T(8,128)} fusion(f32[128,128,39]{1,0,2:T(8,128)} %get-tuple-element.797, f32[39,256]{1,0:T(8,128)S(1)} %bitcast_convert_fusion.25, f32[128,256]{1,0:T(8,128)S(1)} %bitcast_convert_fusion.26, pred[]{:T(512)S(6)} %compare.9, bf16[6,128,256]{1,2,0:T(8,128)(2,1)} %get-tuple-element.810, s32[]{:T(128)} %get-tuple-element.796), kind=kOutput, calls=%fused_computation.34.clone.1 | convolution fusion | flops 330989568 | bytes 5348865 | tf_op jit(solution)/shard_map/while/body/eval_jaxpr/ol,cfl->ocf/dot_general | solution.py:33
  134.3 2.5 fusion.119
  140.2 4.3 %select_add_fusion.4 = f32[128,128,39]{1,0,2:T(8,128)} fusion(f32[128,128,39]{1,0,2:T(8,128)} %get-tuple-element.797, f32[39,256]{1,0:T(8,128)S(1)} %bitcast_convert_fusion.25, f32[128,256]{1,0:T(8,128)S(1)} %bitcast_convert_fusion.26, pred[]{:T(512)S(6)} %compare.9, bf16[6,128,256]{1,2,0:T(8,128)(2,1)} %get-tuple-element.810, s32[]{:T(128)} %get-tuple-element.796), kind=kOutput, calls=%fused_computation.34.clone.1 | convolution fusion | flops 330989568 | bytes 5348865 | tf_op jit(solution)/shard_map/while/body/eval_jaxpr/ol,cfl->ocf/dot_general | solution.py:33
  150.3 4.3 %select_add_fusion.4 = f32[128,128,39]{1,0,2:T(8,128)} fusion(f32[128,128,39]{1,0,2:T(8,128)} %get-tuple-element.797, f32[39,256]{1,0:T(8,128)S(1)} %bitcast_convert_fusion.25, f32[128,256]{1,0:T(8,128)S(1)} %bitcast_convert_fusion.26, pred[]{:T(512)S(6)} %compare.9, bf16[6,128,256]{1,2,0:T(8,128)(2,1)} %get-tuple-element.810, s32[]{:T(128)} %get-tuple-element.796), kind=kOutput, calls=%fused_computation.34.clone.1 | convolution fusion | flops 330989568 | bytes 5348865 | tf_op jit(solution)/shard_map/while/body/eval_jaxpr/ol,cfl->ocf/dot_general | solution.py:33
  163.1 46.5 %while.79 = (s32[]{:T(128)}, f32[128,128,39]{1,0,2:T(8,128)S(1)}, f32[6,128,256]{1,2,0:T(8,128)}, f32[6,39,256]{2,1,0:T(8,128)}, bf16[6,128,256]{1,2,0:T(8,128)(...) while((s32[]{:T(128)}, f32[128,128,39]{1,0,2:T(8,128)S(1)}, ...), condition=%wide.region_19.20_spmd.clone, body=%wide.region_16.19_spmd.clone.sunk | while | flops 663257088 | bytes 13271699 | solution.py:44
  163.3 2.7 select_add_fusion.5
  166.1 2.5 fusion.122
  171.0 2.7 select_add_fusion.5
  173.8 2.5 fusion.122
  178.8 2.7 select_add_fusion.5
  181.6 2.5 fusion.122
  186.6 2.7 select_add_fusion.5
  189.3 2.5 fusion.122
  194.3 2.7 select_add_fusion.5
  197.1 2.5 fusion.122
  202.1 2.8 select_add_fusion.5
  204.8 2.5 fusion.122
  212.3 27.8 %while.80 = (s32[]{:T(128)}, f32[128,39,39]{0,2,1:T(8,128)}, f32[6,39,256]{2,1,0:T(8,128)S(1)}, f32[6,39,256]{2,1,0:T(8,128)}, bf16[6,128,256]{1,2,0:T(8,128)(2,...) while((s32[]{:T(128)}, f32[128,39,39]{0,2,1:T(8,128)}, ...), condition=%wide.region_23.24_spmd.clone, body=%wide.region_20.23_spmd.clone.sunk | while | flops 202076160 | bytes 2577003 | solution.py:44
  249.6 2.6 copy.79
  259.5 5.1 %all-to-all-start.1 = ((bf16[4,2,7680]{2,1,0:T(2,128)(2,1)}), bf16[4,2,7680]{2,1,0:T(2,128)(2,1)S(1)}, u32[]{:S(2)}, u32[]{:S(2)}) async-start(bf16[4,2,7680]{2,1,0:T(2,128)(2,1)} %reshape.220), calls=%async_computation.1 | async-start | bytes 245760 | tf_op jit(solution)/shard_map/all_to_all | solution.py:131
  264.6 6.6 %reduce-scatter.10.cloned.1.call-done = bf16[32,1521]{1,0:T(8,128)(2,1)} async-done(((bf16[128,1521]{1,0:T(8,128)(2,1)}), bf16[32,1521]{1,0:T(8,128)(2,1)}) %reduce-scatter.10.cloned.1.call-update) | async-done | bytes 97360
  273.1 30.4 %reduce-scatter.12.cloned.1.call-done = bf16[32,4992]{1,0:T(8,128)(2,1)} async-done(((bf16[128,4992]{1,0:T(8,128)(2,1)}), bf16[32,4992]{1,0:T(8,128)(2,1)}) %reduce-scatter.12.cloned.1.call-update) | async-done | bytes 319504
  305.7 30.0 %reduce-scatter.14.cloned.1.call-done = bf16[32,4992]{1,0:T(8,128)(2,1)} async-done(((bf16[128,4992]{1,0:T(8,128)(2,1)}), bf16[32,4992]{1,0:T(8,128)(2,1)}) %reduce-scatter.14.cloned.1.call-update) | async-done | bytes 319504
  340.9 71.5 %all-reduce.4.cloned.1.call-done = (bf16[32,1521]{0,1:T(8,128)(2,1)}, bf16[32,4992]{0,1:T(8,128)(2,1)}, bf16[32,4992]{0,1:T(8,128)(2,1)}) async-done(((bf16[32,1521]{0,1:T(8,128)(2,1)}, bf16[32,4992]{0,1:T(8,128)(2,1)}, bf16[32,4992]{0,1:T(8,128)(2,1)}), (bf16[32,1521]{0,1:T(8,128)(2,1)}, bf16[32,4992]{0,1:T(8,128)(2,1)}, bf16[32,4992]{0,1:T(8,128)(2,1)})) %all-reduce.4.cloned.1.call-update) | async-done | bytes 736336 | tf_op jit(solution)/shard_map/psum | solution.py:148
  (281 shorter events, 144.3 us)
Async XLA Ops:
  7.2 1.0 copy-start
  8.1 1.5 copy-start.13
  10.8 18.9 %all-to-all-start = ((bf16[4,2,7680]{2,1,0:T(2,128)(2,1)}), bf16[4,2,7680]{2,1,0:T(2,128)(2,1)S(1)}, u32[]{:S(2)}, u32[]{:S(2)}) async-start(bf16[4,2,7680]{2,1,0:T(2,128)(2,1)} %reshape.218), calls=%async_computation | async-start | bytes 245760 | tf_op jit(solution)/shard_map/all_to_all | solution.py:74
  17.1 254.1 %reduce-scatter.10.cloned.1.call-start = ((), (), s32[]{:S(2)}) async-start(), calls=%async_computation.5 | async-start | bytes 491520
  25.5 3.3 copy-start.10
  25.5 4.2 copy-start.12
  27.4 2.6 copy-start.15
  65.0 30.9 %copy-start.17 = (s32[24]{0:T(128)S(1)}, s32[24]{0:T(128)}, u32[]{:S(2)}) copy-start(s32[24]{0:T(128)} %param.23) | copy-start | bytes 292
  100.4 3.4 copy-start.3
  109.7 4.4 %copy-start.3 = (bf16[128,128,39]{0,1,2:T(8,128)(2,1)S(1)}, bf16[128,128,39]{0,1,2:T(8,128)(2,1)}, u32[]{:S(2)}) copy-start(bf16[128,128,39]{0,1,2:T(8,128)(2,1)} %get-tuple-element.813) | copy-start | bytes 3833860 | tf_op jit(solution)/shard_map/while
  119.8 4.4 %copy-start.3 = (bf16[128,128,39]{0,1,2:T(8,128)(2,1)S(1)}, bf16[128,128,39]{0,1,2:T(8,128)(2,1)}, u32[]{:S(2)}) copy-start(bf16[128,128,39]{0,1,2:T(8,128)(2,1)} %get-tuple-element.813) | copy-start | bytes 3833860 | tf_op jit(solution)/shard_map/while
  130.0 4.4 %copy-start.3 = (bf16[128,128,39]{0,1,2:T(8,128)(2,1)S(1)}, bf16[128,128,39]{0,1,2:T(8,128)(2,1)}, u32[]{:S(2)}) copy-start(bf16[128,128,39]{0,1,2:T(8,128)(2,1)} %get-tuple-element.813) | copy-start | bytes 3833860 | tf_op jit(solution)/shard_map/while
  140.2 4.4 %copy-start.3 = (bf16[128,128,39]{0,1,2:T(8,128)(2,1)S(1)}, bf16[128,128,39]{0,1,2:T(8,128)(2,1)}, u32[]{:S(2)}) copy-start(bf16[128,128,39]{0,1,2:T(8,128)(2,1)} %get-tuple-element.813) | copy-start | bytes 3833860 | tf_op jit(solution)/shard_map/while
  150.3 4.4 %copy-start.3 = (bf16[128,128,39]{0,1,2:T(8,128)(2,1)S(1)}, bf16[128,128,39]{0,1,2:T(8,128)(2,1)}, u32[]{:S(2)}) copy-start(bf16[128,128,39]{0,1,2:T(8,128)(2,1)} %get-tuple-element.813) | copy-start | bytes 3833860 | tf_op jit(solution)/shard_map/while
  163.3 2.8 copy-start.2
  171.0 2.8 copy-start.2
  178.8 2.8 copy-start.2
  186.6 2.8 copy-start.2
  194.3 2.8 copy-start.2
  202.0 2.8 copy-start.2
  240.1 0.7 copy-start.5
  244.9 58.6 %reduce-scatter.12.cloned.1.call-start = ((), (), s32[]{:S(2)}) async-start(), calls=%async_computation.6 | async-start | bytes 1597440
  249.6 2.7 copy-start.1
  252.2 83.5 %reduce-scatter.14.cloned.1.call-start = ((), (), s32[]{:S(2)}) async-start(), calls=%async_computation.7 | async-start | bytes 1597440
  256.1 2.0 copy-start.6
  256.2 2.0 copy-start.7
  256.2 2.0 copy-start.8
  256.2 2.0 copy-start.9
  256.2 2.2 copy-start.16
  259.5 78.5 %all-to-all-start.1 = ((bf16[4,2,7680]{2,1,0:T(2,128)(2,1)}), bf16[4,2,7680]{2,1,0:T(2,128)(2,1)S(1)}, u32[]{:S(2)}, u32[]{:S(2)}) async-start(bf16[4,2,7680]{2,1,0:T(2,128)(2,1)} %reshape.220), calls=%async_computation.1 | async-start | bytes 245760 | tf_op jit(solution)/shard_map/all_to_all | solution.py:131
  264.6 147.7 %all-reduce.4.cloned.1.call-start = ((), (), s32[]{:S(2)}) async-start(), calls=%async_computation.8 | async-start | bytes 5894144 | tf_op jit(solution)/shard_map/psum | solution.py:148
  338.0 0.7 copy-start.14
  412.3 2.4 copy-start.4
  412.3 4.1 copy-start.11
Sparse Core Ops, SparseCore 0:
  245.0 26.1 reduce-scatter.9
  274.1 29.2 reduce-scatter.11
  306.4 29.2 reduce-scatter.13
  338.8 73.5 all-reduce.3
where the time goes:
time: 427 us; the launch traced here: 424 us
  matrix products  151 us (35%)
  waiting for transfers between devices  139 us (33%)
  local copies, waits for them, and re-layouts  86.5 us (20%)
  other arithmetic  17.9 us (4%)
  between operations  14.1 us (3%)
  starting transfers between devices  11.5 us (3%)
    psum x1, waiting for transfers between devices, local(): lax.psum(shares[0].astype(jnp.bfloat16), ('samp', 'col'))  71.5 us
    unnamed x7, waiting for transfers between devices  67.1 us
    dot_general x18, matrix products, accumulate(): jnp.einsum('ol,cfl->ocf', cotangent_part, outer_products, preferred_eleme...  56.2 us
    dot_general x18, matrix products, one_block(): jnp.einsum('ocf,cfl->ol', filter_cube, outer_products, preferred_element_...  50.2 us
    dot_general x18, matrix products, accumulate(): jnp.einsum('ocf,ol->cfl', filter_cube, cotangent_part, preferred_element_...  39.7 us
    dynamic_update_slice x42, local copies, waits for them, and re-layouts, backward_layer(): lax.scan(accumulate, starting, (cotangent, previous, anchor))  31.1 us
    unnamed x49, local copies, waits for them, and re-layouts  27 us
  transfers between devices with their start and end apart: 6, of which 4 were waited for; matrix products, arithmetic and copies ran while one was open for 8% of the time, Pallas kernels for 0%

commit v1 on v0

--- a/solution.py
+++ b/solution.py
@@ -145,7 +145,7 @@
         ).astype(jnp.float32),
     )
     summed = (
-        lax.psum(shares[0].astype(jnp.bfloat16), ("samp", "col")).astype(jnp.float32),
+        lax.psum(lax.psum(shares[0].astype(jnp.bfloat16), "col"), "samp").astype(jnp.float32),
         lax.psum(shares[1].astype(jnp.bfloat16), ("samp", "col")).astype(jnp.float32),
         lax.psum(shares[2].astype(jnp.bfloat16), ("samp", "col")).astype(jnp.float32),
     )

time: 427 us -> 482 us (1.13)
  waiting for transfers between devices: 139 us -> 191 us
    psum x1 -> x3, waiting for transfers between devices: 71.5 us -> 107 us  [the longest x1 68.7 us: local(): lax.psum(shares[1].astype(jnp.bfloat16), ('samp', 'col'))]
    unnamed x7 -> x9, waiting for transfers between devices: 67.1 us -> 83.7 us
    unnamed x49 -> x47, local copies, waits for them, and re-layouts: 27 us -> 28.3 us
  transfers between devices with their start and end apart: 6 -> 8, of which waited for: 4 -> 6; matrix products, arithmetic and copies ran while one was open for 8% -> 8% of each run, Pallas kernels for 0% -> 0%
where the time goes in v1:
time: 482 us; the launch traced here: 478 us
  waiting for transfers between devices  191 us (40%)
  matrix products  149 us (31%)
  local copies, waits for them, and re-layouts  91.1 us (19%)
  other arithmetic  16.4 us (3%)
  between operations  14.4 us (3%)
  starting transfers between devices  11.4 us (2%)
    unnamed x9, waiting for transfers between devices  83.7 us
    psum x1, waiting for transfers between devices, local(): lax.psum(shares[1].astype(jnp.bfloat16), ('samp', 'col'))  68.7 us
    dot_general x18, matrix products, accumulate(): jnp.einsum('ol,cfl->ocf', cotangent_part, outer_products, preferred_eleme...  55.1 us
    dot_general x18, matrix products, one_block(): jnp.einsum('ocf,cfl->ol', filter_cube, outer_products, preferred_element_...  50 us
    dot_general x18, matrix products, accumulate(): jnp.einsum('ocf,ol->cfl', filter_cube, cotangent_part, preferred_element_...  39.5 us
    psum x1, waiting for transfers between devices, local(): lax.psum(lax.psum(shares[0].astype(jnp.bfloat16), 'col'), 'samp')  34.2 us
    dynamic_update_slice x42, local copies, waits for them, and re-layouts, backward_layer(): lax.scan(accumulate, starting, (cotangent, previous, anchor))  31.1 us
    unnamed x47, local copies, waits for them, and re-layouts  28.3 us
  transfers between devices with their start and end apart: 8, of which 6 were waited for; matrix products, arithmetic and copies ran while one was open for 8% of the time, Pallas kernels for 0%

profile of v1, /device:TPU:0, one launch (start us, length us, event | category | flops | bytes accessed | tf_op | source)
XLA Modules:
  0.0 478.1 jit_solution(12594845597933459920)
XLA Ops:
  10.8 6.3 %all-to-all-start = ((bf16[4,2,7680]{2,1,0:T(2,128)(2,1)}), bf16[4,2,7680]{2,1,0:T(2,128)(2,1)S(1)}, u32[]{:S(2)}, u32[]{:S(2)}) async-start(bf16[4,2,7680]{2,1,0:T(2,128)(2,1)} %reshape.218), calls=%async_computation | async-start | bytes 245760 | tf_op jit(solution)/shard_map/all_to_all | solution.py:74
  33.9 9.0 %while.75 = (s32[]{:T(128)}, bf16[6,128,256]{1,2,0:T(8,128)(2,1)S(1)}, bf16[6,39,256]{2,1,0:T(8,128)(2,1)S(1)}, bf16[128,39,39]{0,2,1:T(8,128)(2,1)}, s32[]{:T(128)}) while((s32[]{:T(128)}, bf16[6,128,256]{1,2,0:T(8,128)(2,1)S(1)}, bf16[6,39,256]{2,1,0:T(8,128)(2,1)S(1)}, bf16[128,39,39]{0,2,1:T(8,128)(2,1)}, s32[]{:T(128)}) %tuple.131), condition=%wide.region_1.2_spmd, body=%wide.region_0.1_spmd.sunk | while | flops 100501760 | bytes 596805 | solution.py:25
  43.8 20.9 %while.76 = (s32[]{:T(128)}, bf16[6,128,256]{1,2,0:T(8,128)(2,1)}, bf16[6,128,256]{1,2,0:T(8,128)(2,1)S(1)}, bf16[6,39,256]{2,1,0:T(8,128)(2,1)S(1)}, bf16[128,128,39]{1,0,2:T(8,128)(2,1)}, /*index=5*/s32[]{:T(128)}) while((s32[]{:T(128)}, bf16[6,128,256]{1,2,0:T(8,128)(2,1)}, bf16[6,128,256]{1,2,0:T(8,128)(2,1)S(1)}, ...), condition=%wide.region_5.6_spmd, body=%wide.region_4.5_spmd.sunk | while | flops 329787136 | bytes 1771597 | solution.py:25
  43.8 3.4 fusion.114
  47.3 3.4 fusion.114
  50.8 3.4 fusion.114
  54.3 3.4 fusion.114
  57.7 3.4 fusion.114
  61.2 3.4 fusion.114
  66.6 25.9 %while.77 = (s32[]{:T(128)}, bf16[6,128,256]{1,2,0:T(8,128)(2,1)}, bf16[6,128,256]{1,2,0:T(8,128)(2,1)}, bf16[6,39,256]{2,1,0:T(8,128)(2,1)S(1)}, bf16[128,128,39]{1,0,2:T(8,128)(2,1)}, /*index=5*/s32[]{:T(128)}) while((s32[]{:T(128)}, bf16[6,128,256]{1,2,0:T(8,128)(2,1)}, bf16[6,128,256]{1,2,0:T(8,128)(2,1)}, ...), condition=%wide.region_9.10_spmd, body=%wide.region_8.9_spmd.sunk | while | flops 329787136 | bytes 1771597 | solution.py:25
  67.4 3.4 fusion.116
  71.7 3.4 fusion.116
  76.1 3.4 fusion.116
  80.4 3.4 fusion.116
  84.7 3.4 fusion.116
  89.0 3.4 fusion.116
  93.5 3.7 all-reduce
  100.8 60.1 %while.78 = (s32[]{:T(128)}, f32[128,128,39]{1,0,2:T(8,128)}, f32[6,128,256]{1,2,0:T(8,128)}, f32[6,39,256]{2,1,0:T(8,128)}, bf16[6,128,256]{1,2,0:T(8,128)(2,1)...) while((s32[]{:T(128)}, f32[128,128,39]{1,0,2:T(8,128)}, ...), condition=%wide.region_15.16_spmd.clone, body=%wide.region_12.15_spmd.clone.sunk | while | flops 663257088 | bytes 13271699 | solution.py:44
  101.9 3.4 select_add_fusion.4
  111.1 4.3 select_add_fusion.4
  121.3 4.3 select_add_fusion.4
  131.4 4.3 select_add_fusion.4
  135.8 2.5 fusion.119
  141.6 4.3 select_add_fusion.4
  145.9 2.5 fusion.119
  151.8 4.3 select_add_fusion.4
  156.1 2.5 fusion.119
  164.5 46.5 %while.79 = (s32[]{:T(128)}, f32[128,128,39]{1,0,2:T(8,128)S(1)}, f32[6,128,256]{1,2,0:T(8,128)}, f32[6,39,256]{2,1,0:T(8,128)}, bf16[6,128,256]{1,2,0:T(8,128)(...) while((s32[]{:T(128)}, f32[128,128,39]{1,0,2:T(8,128)S(1)}, ...), condition=%wide.region_19.20_spmd.clone, body=%wide.region_16.19_spmd.clone.sunk | while | flops 663257088 | bytes 13271699 | solution.py:44
  164.7 2.8 select_add_fusion.5
  167.5 2.5 fusion.122
  172.4 2.8 select_add_fusion.5
  175.2 2.5 fusion.122
  180.2 2.7 select_add_fusion.5
  183.0 2.5 fusion.122
  188.0 2.8 select_add_fusion.5
  190.7 2.5 fusion.122
  195.7 2.7 select_add_fusion.5
  203.4 2.7 select_add_fusion.5
  206.2 2.5 fusion.122
  213.7 26.6 %while.80 = (s32[]{:T(128)}, f32[128,39,39]{0,2,1:T(8,128)}, f32[6,39,256]{2,1,0:T(8,128)}, f32[6,39,256]{2,1,0:T(8,128)}, bf16[6,128,256]{1,2,0:T(8,128)(2,1)S(...) while((s32[]{:T(128)}, f32[128,39,39]{0,2,1:T(8,128)}, ...), condition=%wide.region_23.24_spmd.clone, body=%wide.region_20.23_spmd.clone.sunk | while | flops 202076160 | bytes 2543987 | solution.py:44
  244.4 26.3 %reduce-scatter.10.cloned.1.call-done = bf16[32,1521]{1,0:T(8,128)(2,1)} async-done(((bf16[128,1521]{1,0:T(8,128)(2,1)}), bf16[32,1521]{1,0:T(8,128)(2,1)}) %reduce-scatter.10.cloned.1.call-update) | async-done | bytes 97360
  277.3 2.6 copy.79
  287.5 4.5 all-reduce.6.cloned.1.call-done
  293.2 4.9 %all-to-all-start.1 = ((bf16[4,2,7680]{2,1,0:T(2,128)(2,1)}), bf16[4,2,7680]{2,1,0:T(2,128)(2,1)S(1)}, u32[]{:S(2)}, u32[]{:S(2)}) async-start(bf16[4,2,7680]{2,1,0:T(2,128)(2,1)} %reshape.220), calls=%async_computation.1 | async-start | bytes 245760 | tf_op jit(solution)/shard_map/all_to_all | solution.py:131
  298.1 27.4 %reduce-scatter.12.cloned.1.call-done = bf16[32,4992]{1,0:T(8,128)(2,1)} async-done(((bf16[128,4992]{1,0:T(8,128)(2,1)}), bf16[32,4992]{1,0:T(8,128)(2,1)}) %reduce-scatter.12.cloned.1.call-update) | async-done | bytes 319504
  327.7 29.9 %reduce-scatter.14.cloned.1.call-done = bf16[32,4992]{1,0:T(8,128)(2,1)} async-done(((bf16[128,4992]{1,0:T(8,128)(2,1)}), bf16[32,4992]{1,0:T(8,128)(2,1)}) %reduce-scatter.14.cloned.1.call-update) | async-done | bytes 319504
  362.5 34.2 %all-reduce.8.cloned.1.call-done = bf16[32,1521]{0,1:T(8,128)(2,1)} async-done(((bf16[32,1521]{0,1:T(8,128)(2,1)}), bf16[32,1521]{0,1:T(8,128)(2,1)}) %all-reduce.8.cloned.1.call-update) | async-done | bytes 97360 | tf_op jit(solution)/shard_map/psum | solution.py:148
  398.5 68.7 %all-reduce.10.cloned.1.call-done = (bf16[32,4992]{0,1:T(8,128)(2,1)}, bf16[32,4992]{0,1:T(8,128)(2,1)}) async-done(((bf16[32,4992]{0,1:T(8,128)(2,1)}, bf16[32,4992]{0,1:T(8,128)(2,1)}), (bf16[32,4992]{0,1:T(8,128)(2,1)}, bf16[32,4992]{0,1:T(8,128)(2,1)})) %all-reduce.10.cloned.1.call-update) | async-done | bytes 638992 | tf_op jit(solution)/shard_map/psum | solution.py:149
  (285 shorter events, 151.2 us)
Async XLA Ops:
  7.2 1.0 copy-start
  8.1 1.5 copy-start.12
  8.1 9.0 %copy-start.2 = (bf16[128,4992]{1,0:T(8,128)(2,1)S(1)}, bf16[128,4992]{1,0:T(8,128)(2,1)}, u32[]{:S(2)}) copy-start(bf16[128,4992]{1,0:T(8,128)(2,1)} %param.27) | copy-start | bytes 3833860
  10.8 22.2 %all-to-all-start = ((bf16[4,2,7680]{2,1,0:T(2,128)(2,1)}), bf16[4,2,7680]{2,1,0:T(2,128)(2,1)S(1)}, u32[]{:S(2)}, u32[]{:S(2)}) async-start(bf16[4,2,7680]{2,1,0:T(2,128)(2,1)} %reshape.218), calls=%async_computation | async-start | bytes 245760 | tf_op jit(solution)/shard_map/all_to_all | solution.py:74
  17.1 253.5 %reduce-scatter.10.cloned.1.call-start = ((), (), s32[]{:S(2)}) async-start(), calls=%async_computation.7 | async-start | bytes 491520
  28.8 3.3 copy-start.10
  28.8 4.2 copy-start.11
  30.7 2.6 copy-start.14
  66.6 30.9 %copy-start.16 = (s32[24]{0:T(128)S(1)}, s32[24]{0:T(128)}, u32[]{:S(2)}) copy-start(s32[24]{0:T(128)} %param.23) | copy-start | bytes 292
  101.9 3.4 copy-start.4
  111.1 4.3 copy-start.4
  121.3 4.3 copy-start.4
  131.4 4.3 copy-start.4
  141.6 4.3 copy-start.4
  151.7 4.3 copy-start.4
  164.7 2.8 copy-start.3
  172.4 2.8 copy-start.3
  180.2 2.8 copy-start.3
  188.0 2.8 copy-start.3
  195.7 2.8 copy-start.3
  203.4 2.8 copy-start.3
  244.3 47.7 %all-reduce.6.cloned.1.call-start = ((), (), s32[]{:S(2)}) async-start(), calls=%async_computation.5 | async-start | bytes 782336 | tf_op jit(solution)/shard_map/psum | solution.py:148
  272.5 52.9 %reduce-scatter.12.cloned.1.call-start = ((), (), s32[]{:S(2)}) async-start(), calls=%async_computation.8 | async-start | bytes 1597440
  277.3 2.7 copy-start.1
  279.9 77.7 %reduce-scatter.14.cloned.1.call-start = ((), (), s32[]{:S(2)}) async-start(), calls=%async_computation.9 | async-start | bytes 1597440
  284.7 2.6 copy-start.6
  284.7 2.6 copy-start.7
  284.7 2.6 copy-start.8
  284.7 2.6 copy-start.9
  284.7 7.4 %copy-start.15 = (s32[40]{0:T(128)S(1)}, s32[40]{0:T(128)}, u32[]{:S(2)}) copy-start(s32[40]{0:T(128)} %param.22) | copy-start | bytes 484
  287.2 109.4 %all-reduce.8.cloned.1.call-start = ((), (), s32[]{:S(2)}) async-start(), calls=%async_computation.6 | async-start | bytes 782336 | tf_op jit(solution)/shard_map/psum | solution.py:148
  293.2 66.7 %all-to-all-start.1 = ((bf16[4,2,7680]{2,1,0:T(2,128)(2,1)}), bf16[4,2,7680]{2,1,0:T(2,128)(2,1)S(1)}, u32[]{:S(2)}, u32[]{:S(2)}) async-start(bf16[4,2,7680]{2,1,0:T(2,128)(2,1)} %reshape.220), calls=%async_computation.1 | async-start | bytes 245760 | tf_op jit(solution)/shard_map/all_to_all | solution.py:131
  298.1 169.1 %all-reduce.10.cloned.1.call-start = ((), (), s32[]{:S(2)}) async-start(), calls=%async_computation.10 | async-start | bytes 5111808 | tf_op jit(solution)/shard_map/psum | solution.py:149
  327.7 32.6 %copy-start.13 = (s32[1920]{0:T(1024)S(1)}, s32[1920]{0:T(1024)}, u32[]{:S(2)}) copy-start(s32[1920]{0:T(1024)} %copy-done.12) | copy-start | bytes 23044
  467.2 2.4 copy-start.5
Sparse Core Ops, SparseCore 0:
  244.5 26.1 reduce-scatter.9
  273.6 18.3 all-reduce.5
  295.0 30.4 reduce-scatter.11
  328.3 29.2 reduce-scatter.13
  359.8 36.8 all-reduce.7
  399.0 68.1 all-reduce.9
